TPU v7x, 32 devices: a whole 2x2x4 slice. The times are simulated.
32 devices in a mesh: wide: 16 (over z, y, x), narrow: 2 (over core).
Axes of the slice: x: 2, y: 2, z: 4, core: 2. Of those that a mesh axis runs over, the one named last changes fastest.
Arguments:
- contributions: float32 [2, 3, 8192, 128], P('narrow', None, 'wide'), may hold values from -6 to 6
- send_map: int32 [16, 800], P('wide'), may hold values from -1 to 511, as said below
- arrival_map: int32 [16, 800], P('wide'), may hold values from -1 to 255, as said below
- dual_diagonal: float32 [4096, 128], P('wide'), may hold values from 0.5 to 2
- mortar: bfloat16 [4096, 128, 128], P('wide'), may hold values from -0.5 to 0.5
- master_inverse: bfloat16 [4096, 128, 128], P('wide'), may hold values from -0.5 to 0.5
Outputs:
- corrections: float32 [2, 3, 8192, 128], P('narrow', None, 'wide')
Inputs may be any that keep to these rules, and one draw needn't show every extreme that they name: `send_map`: each row 0 to 511 of a partition stands in exactly one of its slots. Some stripe has all 50 of its slots used by every partition. arrival_map[d, o * 50 + c] is -1 exactly where send_map[o, d * 50 + c] is -1.
All inputs are finite; a program needn't handle non-finite values.
Results may differ from a plain program's by a relative error of at most 0.0041.
Values sent between devices are 32-bit elements; how exact they have to be, the bound alone decides.
A program may use at most 64 MiB of HBM per device.

v0:
```python
import jax
import jax.numpy as jnp
from jax import lax
from jax.sharding import PartitionSpec as P


def partner_2(value, axis, stride):
    mask = 2**stride
    pairs = [(source, source ^ mask) for source in range(lax.axis_size(axis))]
    return lax.ppermute(value, axis, pairs)


def condense(slave_sums, master_sums, diagonal, mortar_part, inverse_part):
    multiplier_low = (slave_sums / diagonal[None]).astype(jnp.bfloat16)
    pushed = jnp.einsum(
        "bij,cbi->cbj", mortar_part, multiplier_low, preferred_element_type=jnp.float32
    )
    condensed_low = (master_sums + pushed).astype(jnp.bfloat16)
    master_fix = jnp.einsum(
        "bkj,cbj->cbk", inverse_part, condensed_low, preferred_element_type=jnp.float32
    )
    master_low = master_fix.astype(jnp.bfloat16)
    slave_fix = (
        jnp.einsum("bij,cbj->cbi", mortar_part, master_low, preferred_element_type=jnp.float32)
        / diagonal[None]
    )
    return (slave_fix, master_fix)


def shards(contributions, send_map, arrival_map, dual_diagonal, mortar, master_inverse):
    my_side = lax.axis_index("narrow")
    block_count = dual_diagonal.shape[0]
    node_count = contributions.shape[3]
    comp_count = contributions.shape[1]
    row_count = contributions.shape[2]
    picked = send_map[0]
    is_live = picked >= 0
    filled = jnp.where(is_live, picked, 0)
    outgoing = jnp.take(contributions[0], filled, axis=1) * is_live[None, :, None].astype(
        jnp.float32
    )
    landing = jnp.where(is_live, picked, row_count)
    block_ids = jnp.arange(block_count, dtype=jnp.int32)
    received_rows = lax.all_to_all(outgoing, "wide", split_axis=1, concat_axis=1, tiled=True)
    choosing_mask = (arrival_map[0][:, None] == block_ids[None, :]).astype(jnp.float32)
    local_row_sums = jnp.einsum(
        "gxp,xt->gtp", received_rows, choosing_mask, precision=lax.Precision.HIGHEST
    )
    partner = partner_2(local_row_sums, "narrow", 0)
    slave_sums = jnp.where(my_side == 0, local_row_sums, partner)
    master_sums = jnp.where(my_side == 0, partner, local_row_sums)
    slave_fix, master_fix = condense(slave_sums, master_sums, dual_diagonal, mortar, master_inverse)
    local_correction = jnp.where(my_side == 0, slave_fix, master_fix)
    departing_rows = jnp.einsum(
        "oxq,ux->ouq", local_correction, choosing_mask, precision=lax.Precision.HIGHEST
    )
    returned = lax.all_to_all(departing_rows, "wide", split_axis=1, concat_axis=1, tiled=True)
    placed = (
        jnp.zeros((comp_count, row_count + 1, node_count), jnp.float32)
        .at[:, landing, :]
        .set(returned)
    )
    return placed[:, :row_count][None]


def solution(mesh):
    placed = (
        P("narrow", None, "wide", None),
        P("wide", None),
        P("wide", None),
        P("wide", None),
        P("wide", None, None),
        P("wide", None, None),
    )
    return jax.shard_map(
        shards,
        mesh=mesh,
        in_specs=placed,
        out_specs=P("narrow", None, "wide", None),
        check_vma=False,
    )
```

profile of v0, /device:TPU:0, one launch (start us, length us, event | category | flops | bytes accessed | tf_op | source)
XLA Modules:
  0.0 153.0 jit_solution(14585886316772614351)
XLA Ops:
  0.0 0.7 fusion.21
  0.7 0.7 reduce.2
  1.5 1.7 %copy.37 = f32[1,3,512,128]{3,1,2,0:T(4,128)S(1)} copy(f32[1,3,512,128]{3,2,1,0:T(8,128)} %param.6) | data formatting | bytes 1572864 | tf_op args[0]
  3.1 3.6 %gather_fusion = f32[800,3,128]{2,1,0:T(4,128)S(1)} fusion(f32[3,512,128]{2,0,1:T(4,128)S(1)} %bitcast.35, s32[1024]{0:T(1024)S(1)} %pad_clamp_fusion), kind=kCustom, calls=%fused_computation | custom fusion | bytes 2460800 | tf_op jit(solution)/shard_map/jit(_take)/gather | solution.py:39
  6.8 5.0 %multiply_bitcast_fusion = f32[3,800,128]{2,0,1:T(4,128)} fusion(f32[800,3,128]{2,1,0:T(4,128)S(1)} %gather_fusion, f32[800]{0:T(1024)S(1)} %get-tuple-element.8, pred[800]{0:T(1024)(128)(4,1)S(1)} %get-tuple-element.7), kind=kLoop, calls=%fused_computation.2 | loop fusion | flops 614400 | bytes 2461600 | tf_op jit(solution)/shard_map/mul | solution.py:39
  11.8 0.0 copy-start.1
  11.8 8.5 %all-to-all-start = ((f32[3,800,128]{2,0,1:T(4,128)}), f32[3,800,128]{2,0,1:T(4,128)S(1)}, u32[]{:S(2)}, u32[]{:S(2)}) async-start(f32[3,800,128]{2,0,1:T(4,128)} %multiply_bitcast_fusion), calls=%async_computation | async-start | bytes 3276800 | tf_op jit(solution)/shard_map/all_to_all | solution.py:44
  20.3 0.0 copy-done.1
  20.3 0.0 copy-start
  20.3 35.2 %all-to-all-done = f32[3,800,128]{2,0,1:T(4,128)S(1)} async-done(((f32[3,800,128]{2,0,1:T(4,128)}), f32[3,800,128]{2,0,1:T(4,128)S(1)}, u32[]{:S(2)}, u32[]{:S(2)}) %all-to-all-start) | async-done | bytes 1228832 | tf_op jit(solution)/shard_map/all_to_all | solution.py:44
  55.5 1.2 fusion.4
  56.7 0.1 collective-permute-start
  56.8 1.7 %collective-permute-done = f32[3,256,128]{2,1,0:T(8,128)S(1)} collective-permute-done((f32[3,256,128]{2,1,0:T(8,128)S(1)}, f32[3,256,128]{2,1,0:T(8,128)S(1)}, u32[]{:S(2)}, u32[]{:S(2)}) %collective-permute-start) | collective-permute-done | bytes 393248 | tf_op jit(solution)/shard_map/ppermute | solution.py:10
  58.5 0.0 copy-done
  58.5 0.1 divide_convert_fusion
  58.5 0.0 slice-start
  58.5 5.8 %fusion.17 = f32[256,3,128]{2,1,0:T(4,128)S(1)} fusion(bf16[256,128,128]{2,1,0:T(8,128)(2,1)} %param.10, bf16[3,256,128]{2,1,0:T(8,128)(2,1)S(1)} %divide_convert_fusion), kind=kOutput, calls=%fused_computation.23 | convolution fusion | flops 25165824 | bytes 8978432 | tf_op jit(solution)/shard_map/bij,cbi->cbj/dot_general | solution.py:15
  64.3 0.0 slice-start.1
  64.3 0.1 fusion.12
  64.4 7.9 %fusion.15 = f32[256,3,128]{2,1,0:T(4,128)S(1)} fusion(bf16[256,128,128]{2,1,0:T(8,128)(2,1)} %param.11, bf16[3,256,128]{2,1,0:T(8,128)(2,1)S(1)} %fusion.12), kind=kOutput, calls=%fused_computation.21 | convolution fusion | flops 25165824 | bytes 8978432 | tf_op jit(solution)/shard_map/bkj,cbj->cbk/dot_general | solution.py:19
  72.4 0.0 slice-done
  72.4 0.0 slice-done.1
  72.4 4.4 %fusion.1 = f32[3,256,128]{2,0,1:T(4,128)S(1)} fusion(f32[256,3,128]{2,1,0:T(4,128)S(1)} %fusion.15, bf16[256,128,128]{2,1,0:T(8,128)(2,1)S(1)} %bitcast.33, f32[256,128]{1,0:T(8,128)S(1)} %copy-done, pred[]{:T(512)S(6)} %eq.24), kind=kOutput, calls=%fused_computation.6 | convolution fusion | flops 25460736 | bytes 9306113 | tf_op jit(solution)/shard_map/bij,cbj->cbi/dot_general | solution.py:24
  76.8 0.9 convolution_bitcast_fusion
  77.7 0.8 copy.23
  78.6 48.1 %all_to_all.10 = f32[3,800,128]{2,0,1:T(4,128)S(1)} all-to-all(f32[3,800,128]{2,0,1:T(4,128)S(1)} %copy.23), channel_id=1, replica_groups=mesh['wide'=16,'narrow'=2] {'wide'}, dimensions={1} | all-to-all | bytes 2457600 | tf_op jit(solution)/shard_map/all_to_all | solution.py:57
  126.6 0.1 broadcast_in_dim.28
  126.8 25.1 %scatter_fusion = f32[3,513,128]{2,0,1:T(4,128)S(1)} fusion(f32[3,513,128]{2,0,1:T(4,128)S(1)} %broadcast_in_dim.28, s32[800]{0:T(1024)S(1)} %get-tuple-element.6, f32[800,3,128]{2,1,0:T(4,128)S(1)} %bitcast.34), kind=kCustom, calls=%fused_computation.1 | custom fusion | bytes 3689600 | tf_op jit(solution)/shard_map/scatter | solution.py:61
  151.9 0.2 slice_bitcast_fusion
  152.1 0.9 copy.24
  (4 shorter events, 0.0 us)
Async XLA Ops:
  11.8 8.5 %copy-start.1 = (s32[1,800]{1,0:T(1,128)S(1)}, s32[1,800]{1,0:T(1,128)}, u32[]{:S(2)}) copy-start(s32[1,800]{1,0:T(1,128)} %param.8) | copy-start | bytes 9604
  11.8 43.7 %all-to-all-start = ((f32[3,800,128]{2,0,1:T(4,128)}), f32[3,800,128]{2,0,1:T(4,128)S(1)}, u32[]{:S(2)}, u32[]{:S(2)}) async-start(f32[3,800,128]{2,0,1:T(4,128)} %multiply_bitcast_fusion), calls=%async_computation | async-start | bytes 3276800 | tf_op jit(solution)/shard_map/all_to_all | solution.py:44
  20.3 38.2 %copy-start = (f32[256,128]{1,0:T(8,128)S(1)}, f32[256,128]{1,0:T(8,128)}, u32[]{:S(2)}) copy-start(f32[256,128]{1,0:T(8,128)} %param.9) | copy-start | bytes 393220
  56.7 1.8 %collective-permute-start = (f32[3,256,128]{2,1,0:T(8,128)S(1)}, f32[3,256,128]{2,1,0:T(8,128)S(1)}, u32[]{:S(2)}, u32[]{:S(2)}) collective-permute-start(f32[3,256,128]{2,1,0:T(8,128)S(1)} %fusion.4), channel_id=1, source_target_pairs={{0,1},{1,0},{2,3},{3,2},{4,5},{5,4},{6,7},{7,6},{8,9},{9,8},{10,11... | collective-permute-start | bytes 1179656 | tf_op jit(solution)/shard_map/ppermute | solution.py:10
  58.5 13.8 %slice-start = ((s8[8388608]{0:T(1024)(128)(4,1)}), s8[4194304]{0:T(1024)(128)(4,1)S(1)}, s32[]{:S(2)}) async-start(s8[8388608]{0:T(1024)(128)(4,1)} %bitcast.32), calls=%async_computation.2 | async-start | bytes 8388608
  64.3 8.0 %slice-start.1 = ((s8[8388608]{0:T(1024)(128)(4,1)}), s8[4194304]{0:T(1024)(128)(4,1)S(1)}, s32[]{:S(2)}) async-start(s8[8388608]{0:T(1024)(128)(4,1)} %bitcast.32), calls=%async_computation.3 | async-start | bytes 8388608
where the time goes:
time: 153 us
  blocking collectives  48.1 us (31%)
  waiting for transfers between devices  36.9 us (24%)
  local copies, waits for them, and re-layouts  32.5 us (21%)
  matrix products  20.3 us (13%)
  starting transfers between devices  8.54 us (6%)
  other arithmetic  6.57 us (4%)
    all_to_all x1, blocking collectives, shards(): lax.all_to_all(departing_rows, 'wide', split_axis=1, concat_axis=1, tiled...  48.1 us
    all_to_all x1, waiting for transfers between devices, shards(): lax.all_to_all(outgoing, 'wide', split_axis=1, concat_axis=1, tiled=True)  35.2 us
    scatter x1, local copies, waits for them, and re-layouts, shards(): placed = jnp.zeros((comp_count, row_count + 1, node_count), jnp.float32)....  25.1 us
    all_to_all x1, starting transfers between devices, shards(): lax.all_to_all(outgoing, 'wide', split_axis=1, concat_axis=1, tiled=True)  8.47 us
    dot_general x1, matrix products, condense(): jnp.einsum('bkj,cbj->cbk', inverse_part, condensed_low, preferred_element...  7.93 us
    dot_general x1, matrix products, condense(): jnp.einsum('bij,cbi->cbj', mortar_part, multiplier_low, preferred_element...  5.8 us
    mul x1, other arithmetic, shards(): jnp.take(contributions[0], filled, axis=1)  4.99 us
    dot_general x1, matrix products, condense(): jnp.einsum('bij,cbj->cbi', mortar_part, master_low, preferred_element_typ...  4.45 us
  transfers between devices with their start and end apart: 2, of which 2 were waited for; matrix products, arithmetic and copies ran while one was open for 0% of the time, Pallas kernels for 0%

commit v1 on v0

v1 whole, which is shorter than its diff:
```python
import functools

import jax
import jax.numpy as jnp
from jax import lax
from jax.experimental import pallas as pl
from jax.experimental.pallas import tpu as pltpu
from jax.sharding import PartitionSpec as P

GROUP = 16
SUBLANES = 8


def one_hot_dot(mask, values):
    high = values.astype(jnp.bfloat16)
    low = (values - high.astype(jnp.float32)).astype(jnp.bfloat16)
    return jnp.dot(mask, high, preferred_element_type=jnp.float32) + jnp.dot(
        mask, low, preferred_element_type=jnp.float32
    )


def block_products(vectors, matrices, transposed):
    rows = lax.broadcasted_iota(jnp.int32, vectors.shape, 0)
    total = jnp.zeros(vectors.shape, jnp.float32)
    for b in range(vectors.shape[0]):
        product = lax.dot_general(
            vectors,
            matrices(b),
            (((1,), (1 if transposed else 0,)), ((), ())),
            preferred_element_type=jnp.float32,
        )
        total = jnp.where(rows == b, product, total)
    return total


def kernel(
    n,
    cap,
    contributions,
    send_col,
    send_row,
    arrival_col,
    arrival_row,
    diagonal,
    mortar_hbm,
    inverse_hbm,
    out,
    pick_mask,
    sum_mask,
    spread_mask,
    place_mask,
    going,
    coming,
    returning,
    returned,
    sums,
    other_sums,
    other_fix,
    fixes,
    mortar,
    inverse,
    fetch_sem,
    wide_send,
    wide_recv,
    pair_send,
    pair_recv,
):
    me = lax.axis_index("wide")
    side = lax.axis_index("narrow")
    comps, row_count, nodes = out.shape[1:]
    capp = coming.shape[2]
    slots = n * capp
    half = mortar.shape[0]

    fetches = [
        pltpu.make_async_copy(mortar_hbm.at[pl.ds(side * half, half)], mortar, fetch_sem.at[0]),
        pltpu.make_async_copy(inverse_hbm.at[pl.ds(side * half, half)], inverse, fetch_sem.at[1]),
    ]

    if capp > cap:
        last = pl.ds(capp - SUBLANES, SUBLANES)
        empty = jnp.zeros((comps, n, SUBLANES, nodes), jnp.float32)
        coming[:, :, last, :] = empty
        returned[:, :, last, :] = empty

    barrier = pltpu.get_barrier_semaphore()

    def greet(k, carry):
        pl.semaphore_signal(barrier, inc=1, device_id={"wide": lax.rem(me + k, n)}, device_id_type=pl.DeviceIdType.MESH)
        return carry

    lax.fori_loop(1, n, greet, 0)
    pl.semaphore_signal(barrier, inc=1, device_id={"narrow": 1 - side}, device_id_type=pl.DeviceIdType.MESH)
    for fetch in fetches:
        fetch.start()


    def mask_of(ids, shape, axis):
        return jnp.where(ids == lax.broadcasted_iota(jnp.int32, shape, axis), 1.0, 0.0).astype(jnp.bfloat16)

    def row_mask_of(ids, shape):
        tiles = (shape[0] // SUBLANES, SUBLANES, shape[1])
        rows = lax.broadcasted_iota(jnp.int32, tiles, 0) * SUBLANES + lax.broadcasted_iota(
            jnp.int32, tiles, 1
        )
        return jnp.where(ids[None] == rows, 1.0, 0.0).reshape(shape).astype(jnp.bfloat16)

    pick_mask[...] = mask_of(send_col[...], pick_mask.shape, 1)

    def exchange(source, target, c, phase):
        def one_copy(peer):
            pltpu.make_async_remote_copy(
                src_ref=source.at[c, peer, pl.ds(0, cap)],
                dst_ref=target.at[c, me, pl.ds(0, cap)],
                send_sem=wide_send.at[phase, c],
                recv_sem=wide_recv.at[phase, c],
                device_id={"wide": peer},
                device_id_type=pl.DeviceIdType.MESH,
            ).start()

        middle = n // 2
        one_copy(lax.rem(me + middle, n))

        def pair(k, carry):
            one_copy(lax.rem(me + middle + k, n))
            one_copy(lax.rem(me + middle - k, n))
            return carry

        lax.fori_loop(1, middle, pair, 0)

    def whole(ref, c, sem):
        view = ref.at[c, pl.ds(0, n - 1), pl.ds(0, cap)]
        return pltpu.make_async_copy(view, view, sem)

    for c in range(comps):
        going[c] = one_hot_dot(pick_mask[...], contributions[0, c]).reshape(n, capp, nodes)
        if c == 0:
            pl.semaphore_wait(barrier, n)
        exchange(going, coming, c, 0)
        coming[c, me] = going[c, me]

    sum_mask[...] = row_mask_of(arrival_row[...], sum_mask.shape)
    spread_mask[...] = mask_of(arrival_col[...], spread_mask.shape, 1)
    place_mask[...] = row_mask_of(send_row[...], place_mask.shape)

    mine = pl.multiple_of(side * half, half)
    theirs = pl.multiple_of((1 - side) * half, half)
    is_slave = side == 0

    for c in range(comps):
        whole(coming, c, wide_recv.at[0, c]).wait()
        sums[c] = one_hot_dot(sum_mask[...], coming[c].reshape(slots, nodes))
        swap = pltpu.make_async_remote_copy(
            src_ref=sums.at[c, pl.ds(theirs, half)],
            dst_ref=other_sums.at[c],
            send_sem=pair_send.at[0, c],
            recv_sem=pair_recv.at[0, c],
            device_id={"narrow": 1 - side},
            device_id_type=pl.DeviceIdType.MESH,
        )
        swap.start()
        if c == 0:
            for fetch in fetches:
                fetch.wait()
        swap.wait()

        def condense(g, carry):
            first = pl.multiple_of(g * GROUP, GROUP)
            rows = pl.ds(first, GROUP)
            own = sums[c, pl.ds(pl.multiple_of(mine + first, GROUP), GROUP), :]
            other = other_sums[c, rows, :]
            slave = jnp.where(is_slave, own, other)
            master = jnp.where(is_slave, other, own)
            scale = diagonal[pl.ds(pl.multiple_of(mine + first, GROUP), GROUP), :]
            low = (slave / scale).astype(jnp.bfloat16)
            condensed = master + block_products(low, lambda b: mortar[first + b], False)
            master_fix = block_products(
                condensed.astype(jnp.bfloat16), lambda b: inverse[first + b], True
            )
            slave_fix = (
                block_products(master_fix.astype(jnp.bfloat16), lambda b: mortar[first + b], True)
                / scale
            )
            fixes[c, pl.ds(pl.multiple_of(mine + first, GROUP), GROUP), :] = jnp.where(
                is_slave, slave_fix, master_fix
            )
            other_fix[c, rows, :] = jnp.where(is_slave, master_fix, slave_fix)
            return carry

        lax.fori_loop(0, half // GROUP, condense, 0)
        back = pltpu.make_async_remote_copy(
            src_ref=other_fix.at[c],
            dst_ref=fixes.at[c, pl.ds(mine, half)],
            send_sem=pair_send.at[1, c],
            recv_sem=pair_recv.at[1, c],
            device_id={"narrow": 1 - side},
            device_id_type=pl.DeviceIdType.MESH,
        )
        back.start()
        back.wait()
        returning[c] = one_hot_dot(spread_mask[...], fixes[c]).reshape(n, capp, nodes)
        exchange(returning, returned, c, 1)
        returned[c, me] = returning[c, me]

    for c in range(comps):
        whole(returned, c, wide_recv.at[1, c]).wait()
        out[0, c] = one_hot_dot(place_mask[...], returned[c].reshape(slots, nodes))
    for c in range(comps):
        whole(going, c, wide_send.at[0, c]).wait()
        whole(returning, c, wide_send.at[1, c]).wait()


def shards(contributions, send_map, arrival_map, dual_diagonal, mortar, master_inverse):
    n = lax.axis_size("wide")
    _, comps, row_count, nodes = contributions.shape
    blocks = dual_diagonal.shape[0]
    half = blocks // lax.axis_size("narrow")
    cap = send_map.shape[1] // n
    capp = -(-cap // SUBLANES) * SUBLANES
    slots = n * capp

    def padded(ids):
        return jnp.pad(
            ids.reshape(n, cap), ((0, 0), (0, capp - cap)), constant_values=-1
        )

    send = padded(send_map)
    arrival = padded(arrival_map)
    f32, bf16 = jnp.float32, jnp.bfloat16
    vmem = pl.BlockSpec(memory_space=pltpu.VMEM)
    hbm = pl.BlockSpec(memory_space=pl.ANY)
    travel = pltpu.VMEM((comps, n, capp, nodes), f32)
    return pl.pallas_call(
        functools.partial(kernel, n, cap),
        out_shape=jax.ShapeDtypeStruct((1, comps, row_count, nodes), f32),
        in_specs=[vmem] * 6 + [hbm] * 2,
        out_specs=vmem,
        scratch_shapes=[
            pltpu.VMEM((slots, row_count), bf16),
            pltpu.VMEM((blocks, slots), bf16),
            pltpu.VMEM((slots, blocks), bf16),
            pltpu.VMEM((row_count, slots), bf16),
            travel,
            travel,
            travel,
            travel,
            pltpu.VMEM((comps, blocks, nodes), f32),
            pltpu.VMEM((comps, half, nodes), f32),
            pltpu.VMEM((comps, half, nodes), f32),
            pltpu.VMEM((comps, blocks, nodes), f32),
            pltpu.VMEM((half, nodes, nodes), bf16),
            pltpu.VMEM((half, nodes, nodes), bf16),
            pltpu.SemaphoreType.DMA((2,)),
            pltpu.SemaphoreType.DMA((2, comps)),
            pltpu.SemaphoreType.DMA((2, comps)),
            pltpu.SemaphoreType.DMA((2, comps)),
            pltpu.SemaphoreType.DMA((2, comps)),
        ],
        compiler_params=pltpu.CompilerParams(
            collective_id=0, has_side_effects=True, vmem_limit_bytes=48 * 1024 * 1024
        ),
    )(
        contributions,
        send.reshape(slots, 1),
        jnp.broadcast_to(send.reshape(1, slots), (SUBLANES, slots)),
        arrival.reshape(slots, 1),
        jnp.broadcast_to(arrival.reshape(1, slots), (SUBLANES, slots)),
        dual_diagonal,
        mortar,
        master_inverse,
    )


def solution(mesh):
    placed = (
        P("narrow", None, "wide", None),
        P("wide", None),
        P("wide", None),
        P("wide", None),
        P("wide", None, None),
        P("wide", None, None),
    )
    return jax.shard_map(
        shards,
        mesh=mesh,
        in_specs=placed,
        out_specs=P("narrow", None, "wide", None),
        check_vma=False,
    )
```

time: 153 us -> 71.1 us (0.46)
  Pallas kernels: 0 us -> 65.7 us
  blocking collectives: 48.1 us -> 0 us
  waiting for transfers between devices: 36.9 us -> 0 us
  local copies, waits for them, and re-layouts: 32.5 us -> 3.61 us
  matrix products: 20.3 us -> 0 us
  starting transfers between devices: 8.54 us -> 0 us
  other arithmetic: 6.57 us -> 1.4 us
    pallas_call x0 -> x1, Pallas kernels: none -> 65.7 us  [shards(): pl.pallas_call(functools.partial(kernel, n, cap), out_shape=jax.ShapeDtyp...]
    all_to_all x1 -> x0, blocking collectives: 48.1 us -> none  [shards(): lax.all_to_all(departing_rows, 'wide', split_axis=1, concat_axis=1, tiled...]
    all_to_all x1 -> x0, waiting for transfers between devices: 35.2 us -> none  [shards(): lax.all_to_all(outgoing, 'wide', split_axis=1, concat_axis=1, tiled=True)]
    scatter x1 -> x0, local copies, waits for them, and re-layouts: 25.1 us -> none  [shards(): placed = jnp.zeros((comp_count, row_count + 1, node_count), jnp.float32)....]
    dot_general x5 -> x0, matrix products: 20.3 us -> none  [the longest x1 7.93 us: condense(): jnp.einsum('bkj,cbj->cbk', inverse_part, condensed_low, preferred_element...]
    all_to_all x1 -> x0, starting transfers between devices: 8.47 us -> none  [shards(): lax.all_to_all(outgoing, 'wide', split_axis=1, concat_axis=1, tiled=True)]
    mul x1 -> x0, other arithmetic: 4.99 us -> none  [shards(): jnp.take(contributions[0], filled, axis=1)]
    gather x1 -> x0, local copies, waits for them, and re-layouts: 3.64 us -> none  [shards(): jnp.take(contributions[0], filled, axis=1)]
  transfers between devices with their start and end apart: 2 -> 0, of which waited for: 2 -> 0; matrix products, arithmetic and copies ran while one was open for 0% -> 0% of each run, Pallas kernels for 0% -> 0%
where the time goes in v1:
time: 71.1 us; the launch traced here: 70.8 us
  Pallas kernels  65.7 us (92%)
  local copies, waits for them, and re-layouts  3.61 us (5%)
  other arithmetic  1.4 us (2%)
    pallas_call x1, Pallas kernels, shards(): pl.pallas_call(functools.partial(kernel, n, cap), out_shape=jax.ShapeDtyp...  65.7 us
    unnamed x5, local copies, waits for them, and re-layouts  2.91 us

profile of v1, /device:TPU:0, one launch (start us, length us, event | category | flops | bytes accessed | tf_op | source)
XLA Modules:
  0.0 70.8 jit_solution(17731587128323951948)
XLA Ops:
  0.0 0.7 reduce
  0.7 0.1 reshape.16
  0.8 0.1 broadcast_in_dim.14
  0.9 0.7 reduce.1
  1.6 0.1 reshape.18
  1.7 0.1 broadcast_in_dim.16
  1.8 0.2 reshape.21.arrival_col
  2.0 0.2 reshape.20.send_col
  2.2 0.0 copy-start
  2.2 1.1 %copy-done = f32[1,3,512,128]{3,2,1,0:T(8,128)S(1)} copy-done((f32[1,3,512,128]{3,2,1,0:T(8,128)S(1)}, f32[1,3,512,128]{3,2,1,0:T(8,128)}, u32[]{:S(2)}) %copy-start) | copy-done | bytes 786456
  3.3 0.0 copy-start.1
  3.3 0.9 %copy-done.1 = f32[256,128]{1,0:T(8,128)S(1)} copy-done((f32[256,128]{1,0:T(8,128)S(1)}, f32[256,128]{1,0:T(8,128)}, u32[]{:S(2)}) %copy-start.1) | copy-done | bytes 131096
  4.2 65.7 %shard_map.64 = f32[1,3,512,128]{3,2,1,0:T(8,128)S(1)} custom-call(f32[1,3,512,128]{3,2,1,0:T(8,128)S(1)} %copy-done, s32[896,1]{1,0:T(8,128)S(1)} %reshape.20.send_col, s32[8,896]{1,0:T(8,128)S(1)} %broadcast_in_dim.15.send_row, s32[896,1]{1,0:T(8,128)S(1)} %reshape.21.arrival_col, s32[8,896]{1,0:T(8,128)S(1)} %broadcast_in_dim.17.arrival_row, ...), custom_call_target="tpu_custom_call" | custom-call | tf_op jit(solution)/shard_map/pallas_call | solution.py:233
  70.0 0.9 %copy.10 = f32[1,3,512,128]{3,2,1,0:T(8,128)} copy(f32[1,3,512,128]{3,2,1,0:T(8,128)S(1)} %shard_map.64) | data formatting | bytes 1572864
  (4 shorter events, 0.0 us)
Async XLA Ops:
  2.2 1.1 %copy-start = (f32[1,3,512,128]{3,2,1,0:T(8,128)S(1)}, f32[1,3,512,128]{3,2,1,0:T(8,128)}, u32[]{:S(2)}) copy-start(f32[1,3,512,128]{3,2,1,0:T(8,128)} %contributions.1) | copy-start | bytes 2359300
  3.3 0.9 %copy-start.1 = (f32[256,128]{1,0:T(8,128)S(1)}, f32[256,128]{1,0:T(8,128)}, u32[]{:S(2)}) copy-start(f32[256,128]{1,0:T(8,128)} %diagonal.1) | copy-start | bytes 393220

commit v2 on v1

--- a/solution.py
+++ b/solution.py
@@ -187,7 +187,7 @@
             other_fix[c, rows, :] = jnp.where(is_slave, master_fix, slave_fix)
             return carry
 
-        lax.fori_loop(0, half // GROUP, condense, 0)
+        lax.fori_loop(0, half // GROUP, condense, 0, unroll=2)
         back = pltpu.make_async_remote_copy(
             src_ref=other_fix.at[c],
             dst_ref=fixes.at[c, pl.ds(mine, half)],

time: 71.1 us -> 71 us (level)
  no operation moved by 1% of the time
where the time goes in v2:
time: 71 us; the launch traced here: 70.8 us
  Pallas kernels  65.7 us (93%)
  local copies, waits for them, and re-layouts  3.61 us (5%)
  other arithmetic  1.4 us (2%)
    pallas_call x1, Pallas kernels, shards(): pl.pallas_call(functools.partial(kernel, n, cap), out_shape=jax.ShapeDtyp...  65.7 us
    unnamed x5, local copies, waits for them, and re-layouts  2.91 us

profile of v2, /device:TPU:0, one launch (start us, length us, event | category | flops | bytes accessed | tf_op | source)
XLA Modules:
  0.0 70.8 jit_solution(6477542949376583943)
XLA Ops:
  0.0 0.7 reduce
  0.7 0.1 reshape.16
  0.8 0.1 broadcast_in_dim.14
  0.9 0.7 reduce.1
  1.6 0.1 reshape.18
  1.7 0.1 broadcast_in_dim.16
  1.8 0.2 reshape.21.arrival_col
  2.0 0.2 reshape.20.send_col
  2.2 0.0 copy-start
  2.2 1.1 %copy-done = f32[1,3,512,128]{3,2,1,0:T(8,128)S(1)} copy-done((f32[1,3,512,128]{3,2,1,0:T(8,128)S(1)}, f32[1,3,512,128]{3,2,1,0:T(8,128)}, u32[]{:S(2)}) %copy-start) | copy-done | bytes 786456
  3.3 0.0 copy-start.1
  3.3 0.9 %copy-done.1 = f32[256,128]{1,0:T(8,128)S(1)} copy-done((f32[256,128]{1,0:T(8,128)S(1)}, f32[256,128]{1,0:T(8,128)}, u32[]{:S(2)}) %copy-start.1) | copy-done | bytes 131096
  4.2 65.7 %shard_map.64 = f32[1,3,512,128]{3,2,1,0:T(8,128)S(1)} custom-call(f32[1,3,512,128]{3,2,1,0:T(8,128)S(1)} %copy-done, s32[896,1]{1,0:T(8,128)S(1)} %reshape.20.send_col, s32[8,896]{1,0:T(8,128)S(1)} %broadcast_in_dim.15.send_row, s32[896,1]{1,0:T(8,128)S(1)} %reshape.21.arrival_col, s32[8,896]{1,0:T(8,128)S(1)} %broadcast_in_dim.17.arrival_row, ...), custom_call_target="tpu_custom_call" | custom-call | tf_op jit(solution)/shard_map/pallas_call | solution.py:233
  69.9 0.9 %copy.10 = f32[1,3,512,128]{3,2,1,0:T(8,128)} copy(f32[1,3,512,128]{3,2,1,0:T(8,128)S(1)} %shard_map.64) | data formatting | bytes 1572864
  (4 shorter events, 0.0 us)
Async XLA Ops:
  2.2 1.1 %copy-start = (f32[1,3,512,128]{3,2,1,0:T(8,128)S(1)}, f32[1,3,512,128]{3,2,1,0:T(8,128)}, u32[]{:S(2)}) copy-start(f32[1,3,512,128]{3,2,1,0:T(8,128)} %contributions.1) | copy-start | bytes 2359300
  3.3 0.9 %copy-start.1 = (f32[256,128]{1,0:T(8,128)S(1)}, f32[256,128]{1,0:T(8,128)}, u32[]{:S(2)}) copy-start(f32[256,128]{1,0:T(8,128)} %diagonal.1) | copy-start | bytes 393220
